TPU v7x, 128 devices: a whole 4x4x4 slice. The times are simulated.
128 devices in a mesh: fsdp: 64 (over z, y, x), ep: 2 (over core).
Axes of the slice: x: 4, y: 4, z: 4, core: 2. Of those that a mesh axis runs over, the one named last changes fastest.
Arguments:
- x_tok: bfloat16 [262144, 512], P(('fsdp', 'ep'))
- dy_tok: bfloat16 [262144, 512], P(('fsdp', 'ep'))
- expert_idx: int32 [262144, 4], P(('fsdp', 'ep'))
- gate_val: float32 [262144, 4], P(('fsdp', 'ep'))
- w_one: bfloat16 [60, 512, 352], P('ep', 'fsdp')
- w_two: bfloat16 [60, 352, 512], P('ep', None, 'fsdp')
- w_three: bfloat16 [60, 512, 352], P('ep', 'fsdp')
- ws_one: bfloat16 [512, 1408], P('fsdp')
- ws_two: bfloat16 [1408, 512], P(None, 'fsdp')
- ws_three: bfloat16 [512, 1408], P('fsdp')
Outputs:
- output 1: bfloat16 [262144, 512], P(('fsdp', 'ep'))
- output 2: float32 [262144, 4], P(('fsdp', 'ep'))
- output 3: float32 [60, 512, 352], P('ep', 'fsdp')
- output 4: float32 [60, 352, 512], P('ep', None, 'fsdp')
- output 5: float32 [60, 512, 352], P('ep', 'fsdp')
- output 6: float32 [512, 1408], P('fsdp')
- output 7: float32 [1408, 512], P(None, 'fsdp')
- output 8: float32 [512, 1408], P('fsdp')
All inputs are finite; a program needn't handle non-finite values.
Results may differ from a plain program's by a relative error of at most 0.0058101.
Values are sent between devices in bfloat16 or wider.
A program may use at most 1 GiB of HBM per device.

v0:
```python
import jax
import jax.numpy as jnp
from jax import lax
from jax.sharding import PartitionSpec as P

CAP_NUM = 5
CAP_DEN = 4


def capacity_for(tok_dev, top_k, n_exp):
    needed = -(-(tok_dev * top_k * CAP_NUM) // (CAP_DEN * n_exp))
    return max(8, -(-needed // 8) * 8)


def route_slots(ids_dev, n_exp, capacity):
    flat_ids = ids_dev.reshape(-1)
    n_assign = flat_ids.shape[0]
    onehot = (flat_ids[:, None] == jnp.arange(n_exp, dtype=jnp.int32)[None, :]).astype(jnp.int32)
    slot_pos = jnp.sum(jnp.cumsum(onehot, axis=0) * onehot, axis=1) - 1
    slot_idx = jnp.where(slot_pos < capacity, flat_ids * capacity + slot_pos, n_exp * capacity)
    filled = jnp.full((n_exp * capacity + 1,), n_assign, jnp.int32)
    filled = filled.at[slot_idx].set(jnp.arange(n_assign, dtype=jnp.int32))
    return slot_idx, filled[: n_exp * capacity]


def swiglu_backward(x_rows, g_rows, w_a, w_b, w_c, lead_dims, batch_dim):
    up_form = lead_dims + "d," + batch_dim + "df->" + lead_dims + "f"
    back_form = lead_dims + "d," + batch_dim + "fd->" + lead_dims + "f"
    into_form = lead_dims + "f," + batch_dim + "df->" + lead_dims + "d"
    grad_in = lead_dims + "d," + lead_dims + "f->" + batch_dim + "df"
    grad_out = lead_dims + "f," + lead_dims + "d->" + batch_dim + "fd"
    h_one = jnp.einsum(up_form, x_rows, w_a, preferred_element_type=jnp.float32)
    h_three = jnp.einsum(up_form, x_rows, w_c, preferred_element_type=jnp.float32)
    sig_one = jax.nn.sigmoid(h_one)
    silu_one = h_one * sig_one
    act_rows = (silu_one * h_three).astype(jnp.bfloat16)
    d_act = jnp.einsum(back_form, g_rows, w_b, preferred_element_type=jnp.float32)
    dh_one = (d_act * h_three * sig_one * (1.0 + h_one * (1.0 - sig_one))).astype(jnp.bfloat16)
    dh_three = (d_act * silu_one).astype(jnp.bfloat16)
    dx_rows = (jnp.einsum(into_form, dh_one, w_a, preferred_element_type=jnp.float32) + jnp.einsum(into_form, dh_three, w_c, preferred_element_type=jnp.float32)).astype(jnp.bfloat16)
    dw_a = jnp.einsum(grad_in, x_rows, dh_one, preferred_element_type=jnp.float32)
    dw_b = jnp.einsum(grad_out, act_rows, g_rows, preferred_element_type=jnp.float32)
    dw_c = jnp.einsum(grad_in, x_rows, dh_three, preferred_element_type=jnp.float32)
    return dx_rows, act_rows, dw_a, dw_b, dw_c


def solution(mesh):
    ep_size = mesh.shape["ep"]
    tok_spec = P(("fsdp", "ep"), None)
    in_specs = (tok_spec, tok_spec, tok_spec, tok_spec, P("ep", "fsdp", None), P("ep", None, "fsdp"), P("ep", "fsdp", None), P("fsdp", None), P(None, "fsdp"), P("fsdp", None))
    out_specs = (tok_spec, tok_spec, P("ep", "fsdp", None), P("ep", None, "fsdp"), P("ep", "fsdp", None), P("fsdp", None), P(None, "fsdp"), P("fsdp", None))

    def device_step(x_loc, dy_loc, ids_loc, gate_loc, w_one, w_two, w_three, ws_one, ws_two, ws_three):
        tok_dev, top_k = ids_loc.shape
        model_dim = x_loc.shape[1]
        n_local = w_one.shape[0]
        n_exp = n_local * ep_size
        capacity = capacity_for(tok_dev, top_k, n_exp)
        slot_idx, filled = route_slots(ids_loc, n_exp, capacity)
        zero_row = jnp.zeros((1, model_dim), jnp.bfloat16)
        zero_one = jnp.zeros((1,), jnp.float32)
        tok_src = filled // top_k
        buf_shape = (ep_size, n_local, capacity, model_dim)
        x_send = jnp.concatenate([x_loc, zero_row])[tok_src].reshape(buf_shape)
        dy_send = jnp.concatenate([dy_loc, zero_row])[tok_src].reshape(buf_shape)
        gate_send = jnp.concatenate([gate_loc.reshape(-1), zero_one])[filled].reshape(buf_shape[:3])
        x_recv = lax.all_to_all(x_send, "ep", 0, 0, tiled=True)
        dy_recv = lax.all_to_all(dy_send, "ep", 0, 0, tiled=True)
        gate_recv = lax.all_to_all(gate_send, "ep", 0, 0, tiled=True)
        w_one_full = lax.all_gather(w_one, "fsdp", axis=1, tiled=True)
        w_three_full = lax.all_gather(w_three, "fsdp", axis=1, tiled=True)
        w_two_full = lax.all_gather(w_two, "fsdp", axis=2, tiled=True)
        ws_one_full = lax.all_gather(ws_one, "fsdp", axis=0, tiled=True)
        ws_three_full = lax.all_gather(ws_three, "fsdp", axis=0, tiled=True)
        ws_two_full = lax.all_gather(ws_two, "fsdp", axis=1, tiled=True)
        dy_wide = dy_recv.astype(jnp.float32)
        g_recv = (gate_recv[..., None] * dy_wide).astype(jnp.bfloat16)
        dx_recv, act_recv, dw_one, dw_two, dw_three = swiglu_backward(x_recv, g_recv, w_one_full, w_two_full, w_three_full, "sec", "e")
        y_recv = jnp.einsum("secf,efd->secd", act_recv, w_two_full, preferred_element_type=jnp.float32)
        dgate_recv = jnp.sum(dy_wide * y_recv, axis=-1)
        dx_back = lax.all_to_all(dx_recv, "ep", 0, 0, tiled=True).reshape(n_exp * capacity, model_dim)
        dgate_back = lax.all_to_all(dgate_recv, "ep", 0, 0, tiled=True).reshape(-1)
        dx_assign = jnp.concatenate([dx_back, zero_row])[slot_idx].reshape(tok_dev, top_k, model_dim)
        dgate_loc = jnp.concatenate([dgate_back, zero_one])[slot_idx].reshape(tok_dev, top_k)
        shared_out = swiglu_backward(x_loc, dy_loc, ws_one_full, ws_two_full, ws_three_full, "t", "")
        dx_loc = (jnp.sum(dx_assign.astype(jnp.float32), axis=1) + shared_out[0].astype(jnp.float32)).astype(jnp.bfloat16)
        dw_one = lax.psum_scatter(dw_one, "fsdp", scatter_dimension=1, tiled=True)
        dw_three = lax.psum_scatter(dw_three, "fsdp", scatter_dimension=1, tiled=True)
        dw_two = lax.psum_scatter(dw_two, "fsdp", scatter_dimension=2, tiled=True)
        dws_one = lax.psum(lax.psum_scatter(shared_out[2], "fsdp", scatter_dimension=0, tiled=True), "ep")
        dws_two = lax.psum(lax.psum_scatter(shared_out[3], "fsdp", scatter_dimension=1, tiled=True), "ep")
        dws_three = lax.psum(lax.psum_scatter(shared_out[4], "fsdp", scatter_dimension=0, tiled=True), "ep")
        return dx_loc, dgate_loc, dw_one, dw_two, dw_three, dws_one, dws_two, dws_three

    return jax.shard_map(device_step, mesh=mesh, in_specs=in_specs, out_specs=out_specs, check_vma=False)
```

profile of v0, /device:TPU:1, one launch (start us, length us, event | category | flops | bytes accessed | tf_op | source)
XLA Modules:
  0.0 1484.6 jit_solution(12025489628130464557)
XLA Ops:
  9.4 66.9 %all-gather.17.cloned.1.call-done = bf16[512,1408]{1,0:T(8,128)(2,1)} async-done(((bf16[8,1408]{1,0:T(8,128)(2,1)}), bf16[512,1408]{1,0:T(8,128)(2,1)}) %all-gather.17.cloned.1.call-update) | async-done | bytes 1441808 | tf_op jit(solution)/shard_map/all_gather | solution.py:73
  76.3 9.7 fusion.45
  86.1 54.9 %all-gather.15.cloned.1.call-done = bf16[512,1408]{1,0:T(8,128)(2,1)} async-done(((bf16[8,1408]{1,0:T(8,128)(2,1)}), bf16[512,1408]{1,0:T(8,128)(2,1)}) %all-gather.15.cloned.1.call-update) | async-done | bytes 1441808 | tf_op jit(solution)/shard_map/all_gather | solution.py:74
  149.2 9.9 fusion.33
  159.1 46.5 %all-gather.13.cloned.1.call-done = bf16[1408,512]{0,1:T(8,128)(2,1)} async-done(((bf16[1408,8]{0,1:T(8,128)(2,1)}), bf16[1408,512]{0,1:T(8,128)(2,1)}) %all-gather.13.cloned.1.call-update) | async-done | bytes 1441808 | tf_op jit(solution)/shard_map/all_gather | solution.py:75
  205.6 14.8 multiply_convert_fusion.1
  220.4 9.5 convolution_bitcast_fusion.4
  239.9 32.2 %reduce-window.6 = s32[60,64,128]{2,1,0:T(8,128)S(1)} reduce-window(s32[60,64,128]{2,1,0:T(8,128)} %fusion.38, s32[]{:T(128)} %constant.12.clone.1), window={size=1x1x128 pad=0_0x0_0x127_0}, to_apply=%region_0.0 | reduce-window | flops 62423040 | bytes 3932164 | tf_op jit(solution)/shard_map/reduce-window
  279.4 30.5 %scatter_custom_fusion = s32[10561]{0:T(1024)S(1)} fusion(s32[8192]{0:T(1024)S(1)} %bitcast.125, s32[8192]{0:T(1024)S(1)} %iota.11, s32[]{:T(128)} %constant.16.clone.1), kind=kCustom, calls=%fused_computation.78 | custom fusion | bytes 42248 | tf_op jit(solution)/shard_map/scatter | solution.py:22
  310.0 54.6 %gather_fusion = f32[10560]{0:T(1024)S(1)} fusion(f32[8193]{0:T(1024)S(1)} %pad_maximum_fusion.1, s32[11264]{0:T(1024)S(1)} %get-tuple-element.54), kind=kCustom, calls=%fused_computation | custom fusion | bytes 126720 | tf_op jit(solution)/shard_map/gather | solution.py:66
  374.5 32.9 %gather_fusion.2 = bf16[10560,512]{1,0:T(8,128)(2,1)} fusion(bf16[2049,512]{1,0:T(8,128)(2,1)} %concatenate.17, s32[11264]{0:T(1024)S(1)} %get-tuple-element.53), kind=kCustom, calls=%fused_computation.2 | custom fusion | bytes 21669120 | tf_op jit(solution)/shard_map/gather | solution.py:64
  407.4 30.6 %gather_fusion.1 = bf16[10560,512]{1,0:T(8,128)(2,1)} fusion(bf16[2049,512]{1,0:T(8,128)(2,1)S(1)} %concatenate.16, s32[11264]{0:T(1024)S(1)} %get-tuple-element.53), kind=kCustom, calls=%fused_computation.1 | custom fusion | bytes 21669120 | tf_op jit(solution)/shard_map/gather | solution.py:65
  463.8 36.2 %all-gather.11.cloned.1.call-done = bf16[30,512,352]{2,1,0:T(8,128)(2,1)} async-done(((bf16[30,8,352]{2,1,0:T(8,128)(2,1)}), bf16[30,512,352]{2,1,0:T(8,128)(2,1)}) %all-gather.11.cloned.1.call-update) | async-done | bytes 10813456 | tf_op jit(solution)/shard_map/all_gather | solution.py:70
  500.0 15.3 %fusion.13 = f32[30,2,176,352]{3,2,1,0:T(8,128)} fusion(bf16[30,512,352]{2,1,0:T(8,128)(2,1)} %all-gather.11.cloned.1.call-done, bf16[2,30,176,512]{3,2,1,0:T(8,128)(2,1)} %all-to-all-done.2), kind=kOutput, calls=%fused_computation.28 | convolution fusion | flops 3806330880 | bytes 36495360 | tf_op jit(solution)/shard_map/secd,edf->secf/dot_general | solution.py:32
  515.3 80.4 %all-gather.7.cloned.1.call-done = bf16[30,352,512]{1,2,0:T(8,128)(2,1)} async-done(((bf16[30,352,8]{1,2,0:T(8,128)(2,1)}), bf16[30,352,512]{1,2,0:T(8,128)(2,1)}) %all-gather.7.cloned.1.call-update) | async-done | bytes 10813456 | tf_op jit(solution)/shard_map/all_gather | solution.py:72
  595.7 15.4 %fusion.17 = f32[30,2,176,352]{3,2,1,0:T(8,128)} fusion(bf16[30,352,512]{1,2,0:T(8,128)(2,1)} %all-gather.7.cloned.1.call-done, f32[2,30,176]{2,0,1:T(2,128)S(1)} %copy.50, bf16[2,30,176,512]{3,2,1,0:T(8,128)(2,1)} %all-to-all-done.1), kind=kOutput, calls=%fused_computation.32 | convolution fusion | flops 3822551040 | bytes 36537600 | tf_op jit(solution)/shard_map/secd,efd->secf/dot_general | solution.py:37
  611.0 80.4 %all-gather.9.cloned.1.call-done = bf16[30,512,352]{2,1,0:T(8,128)(2,1)} async-done(((bf16[30,8,352]{2,1,0:T(8,128)(2,1)}), bf16[30,512,352]{2,1,0:T(8,128)(2,1)}) %all-gather.9.cloned.1.call-update) | async-done | bytes 10813456 | tf_op jit(solution)/shard_map/all_gather | solution.py:71
  691.5 27.9 %fusion.9 = (bf16[2,30,176,352]{3,2,0,1:T(8,128)(2,1)}, bf16[2,30,176,352]{3,2,0,1:T(8,128)(2,1)}, bf16[2,30,176,352]{3,2,0,1:T(8,128)(2,1)}) fusion(f32[30,2,176,352]{3,2,1,0:T(8,128)} %fusion.13, f32[30,2,176,352]{3,2,1,0:T(8,128)} %fusion.17, bf16[30,512,352]{2,1,0:T(8,128)(2,1)} %all-gather.9.cloned.1.call-done, ...), kind=kOutput, calls=%fused_computation.23 | convolution fusion | flops 3862087680 | bytes 73666560 | tf_op jit(solution)/shard_map/secd,edf->secf/dot_general | solution.py:33
  719.4 17.1 %convolution_bitcast_fusion.1 = f32[30,512,352]{2,1,0:T(8,128)} fusion(bf16[2,30,176,512]{3,2,1,0:T(8,128)(2,1)} %all-to-all-done.2, bf16[2,30,176,352]{3,2,0,1:T(8,128)(2,1)} %get-tuple-element.47), kind=kOutput, calls=%fused_computation.47 | convolution fusion | flops 3806330880 | bytes 39874560 | tf_op jit(solution)/shard_map/secd,secf->edf/dot_general | solution.py:41
  736.6 19.8 %convolution_bitcast_fusion.2 = f32[30,352,512]{1,2,0:T(8,128)} fusion(bf16[2,30,176,352]{3,2,0,1:T(8,128)(2,1)} %get-tuple-element.46, f32[2,30,176]{2,0,1:T(2,128)S(1)} %copy.50, bf16[2,30,176,512]{3,2,1,0:T(8,128)(2,1)} %all-to-all-done.1), kind=kOutput, calls=%fused_computation.48 | convolution fusion | flops 3822551040 | bytes 39916800 | tf_op jit(solution)/shard_map/secf,secd->efd/dot_general | solution.py:42
  756.5 17.1 %convolution_bitcast_fusion = f32[30,512,352]{2,1,0:T(8,128)} fusion(bf16[2,30,176,512]{3,2,1,0:T(8,128)(2,1)} %all-to-all-done.2, bf16[2,30,176,352]{3,2,0,1:T(8,128)(2,1)} %get-tuple-element.48), kind=kOutput, calls=%fused_computation.46 | convolution fusion | flops 3806330880 | bytes 39874560 | tf_op jit(solution)/shard_map/secd,secf->edf/dot_general | solution.py:43
  786.6 14.1 fusion.11
  800.7 19.3 %fusion.24 = bf16[2,30,176,512]{3,2,0,1:T(8,128)(2,1)} fusion(f32[30,2,176,512]{3,2,1,0:T(8,128)} %fusion.11, bf16[2,30,176,352]{3,2,0,1:T(8,128)(2,1)} %get-tuple-element.48, bf16[30,512,352]{2,1,0:T(8,128)(2,1)} %all-gather.9.cloned.1.call-done), kind=kOutput, calls=%fused_computation.43 | convolution fusion | flops 3817144320 | bytes 50688000 | tf_op jit(solution)/shard_map/secf,edf->secd/dot_general | solution.py:40
  825.7 14.5 all_to_all.25
  844.7 39.4 %gather_fusion.3 = bf16[8192,512]{1,0:T(8,128)(2,1)} fusion(bf16[10561,512]{1,0:T(8,128)(2,1)} %concatenate.18, s32[8192]{0:T(1024)S(1)} %broadcast_clamp_fusion), kind=kCustom, calls=%fused_computation.3 | custom fusion | bytes 16809984 | tf_op jit(solution)/shard_map/gather | solution.py:83
  884.2 15.5 %reshape.106 = f32[2048,4,512]{2,1,0:T(4,128)} reshape(bf16[8192,512]{1,0:T(8,128)(2,1)} %gather_fusion.3) | data formatting | bytes 25165824 | tf_op jit(solution)/shard_map/convert_element_type | solution.py:86
  899.6 12.5 fusion.1
  916.1 45.5 %gather_fusion.4 = f32[8192]{0:T(1024)S(1)} fusion(f32[10561]{0:T(1024)S(1)} %pad_maximum_fusion, s32[8192]{0:T(1024)S(1)} %broadcast_clamp_fusion), kind=kCustom, calls=%fused_computation.4 | custom fusion | bytes 98304 | tf_op jit(solution)/shard_map/gather | solution.py:84
  963.7 16.2 %reduce_sum.28 = f32[2048,512]{1,0:T(8,128)} reduce(f32[2048,4,512]{2,1,0:T(4,128)} %reshape.106, f32[]{:T(128)} %constant.45.clone.1), dimensions={1}, to_apply=%region_4.5 | reduce | flops 3145728 | bytes 20971524 | tf_op jit(solution)/shard_map/reduce_sum | solution.py:86
  979.9 8.6 add_convert_fusion.1
  988.5 239.6 %reduce-scatter.8.cloned.1.call-done = f32[30,352,8]{1,2,0:T(8,128)} async-done(((f32[30,352,512]{1,2,0:T(8,128)}), f32[30,352,8]{1,2,0:T(8,128)}) %reduce-scatter.8.cloned.1.call-update) | async-done | bytes 337936 | tf_op jit(solution)/shard_map/reduce_scatter | solution.py:89
  1228.0 248.9 %reduce-scatter.10.cloned.1.call-done = f32[30,8,352]{2,1,0:T(8,128)} async-done(((f32[30,512,352]{2,1,0:T(8,128)}), f32[30,8,352]{2,1,0:T(8,128)}) %reduce-scatter.10.cloned.1.call-update) | async-done | bytes 337936 | tf_op jit(solution)/shard_map/reduce_scatter | solution.py:88
  (100 shorter events, 92.6 us)
Async XLA Ops:
  7.2 133.8 %copy-start = (bf16[2048,512]{1,0:T(8,128)(2,1)S(1)}, bf16[2048,512]{1,0:T(8,128)(2,1)}, u32[]{:S(2)}) copy-start(bf16[2048,512]{1,0:T(8,128)(2,1)} %param.10) | copy-start | bytes 6291460
  7.2 69.2 %all-gather.17.cloned.1.call-start = ((), (), s32[]{:S(2)}) async-start(), calls=%async_computation.13 | async-start | bytes 1464320 | tf_op jit(solution)/shard_map/all_gather | solution.py:73
  7.9 133.0 %all-gather.15.cloned.1.call-start = ((), (), s32[]{:S(2)}) async-start(), calls=%async_computation.12 | async-start | bytes 1464320 | tf_op jit(solution)/shard_map/all_gather | solution.py:74
  8.7 196.9 %all-gather.13.cloned.1.call-start = ((), (), s32[]{:S(2)}) async-start(), calls=%async_computation.11 | async-start | bytes 1464320 | tf_op jit(solution)/shard_map/all_gather | solution.py:75
  9.4 437.9 %all-reduce.11.cloned.1.call-start = ((), (), s32[]{:S(2)}) async-start(), calls=%async_computation.17 | async-start | bytes 17301504
  141.0 8.2 copy-start.2
  141.0 8.2 copy-start.11
  220.4 9.5 copy-start.12
  229.9 6.8 copy-start.3
  234.8 265.2 %all-gather.11.cloned.1.call-start = ((), (), s32[]{:S(2)}) async-start(), calls=%async_computation.10 | async-start | bytes 11980800 | tf_op jit(solution)/shard_map/all_gather | solution.py:70
  235.4 360.3 %all-gather.7.cloned.1.call-start = ((), (), s32[]{:S(2)}) async-start(), calls=%async_computation.8 | async-start | bytes 11980800 | tf_op jit(solution)/shard_map/all_gather | solution.py:72
  235.9 455.5 %all-gather.9.cloned.1.call-start = ((), (), s32[]{:S(2)}) async-start(), calls=%async_computation.9 | async-start | bytes 11980800 | tf_op jit(solution)/shard_map/all_gather | solution.py:71
  238.3 39.1 %copy-start.7 = (f32[2048,4]{0,1:T(4,128)S(1)}, f32[2048,4]{0,1:T(4,128)}, u32[]{:S(2)}) copy-start(f32[2048,4]{0,1:T(4,128)} %param.13) | copy-start | bytes 98308
  278.8 0.6 copy-start.4
  310.0 61.2 %copy-start.1 = (bf16[2048,512]{1,0:T(8,128)(2,1)S(1)}, bf16[2048,512]{1,0:T(8,128)(2,1)}, u32[]{:S(2)}) copy-start(bf16[2048,512]{1,0:T(8,128)(2,1)} %param.10) | copy-start | bytes 6291460
  365.3 73.9 %all-to-all-start = ((f32[2,30,176]{2,1,0:T(8,128)}), f32[2,30,176]{2,1,0:T(8,128)S(1)}, u32[]{:S(2)}, u32[]{:S(2)}) async-start(f32[2,30,176]{2,1,0:T(8,128)} %reshape.100), calls=%async_computation | async-start | bytes 131072 | tf_op jit(solution)/shard_map/all_to_all | solution.py:69
  407.4 30.6 %copy-start.10 = (u32[128]{0:T(128)S(1)}, u32[128]{0:T(128)}, u32[]{:S(2)}) copy-start(u32[128]{0:T(128)} %constant.60) | copy-start | bytes 1540
  439.2 16.4 %all-to-all-start.2 = ((bf16[2,30,176,512]{3,2,1,0:T(8,128)(2,1)}), bf16[2,30,176,512]{3,2,1,0:T(8,128)(2,1)}, u32[]{:S(2)}, u32[]{:S(2)}) async-start(bf16[2,30,176,512]{3,2,1,0:T(8,128)(2,1)} %bitcast.121), calls=%async_computation.2 | async-start | bytes 21626880 | tf_op jit(solution)/shard_map/all_to_all | solution.py:67
  447.2 335.5 %all-reduce.13.cloned.1.call-start = ((), (), s32[]{:S(2)}) async-start(), calls=%async_computation.18 | async-start | bytes 2973696 | tf_op jit(solution)/shard_map/psum | solution.py:90
  455.7 59.6 %all-to-all-start.1 = ((bf16[2,30,176,512]{3,2,1,0:T(8,128)(2,1)}), bf16[2,30,176,512]{3,2,1,0:T(8,128)(2,1)}, u32[]{:S(2)}, u32[]{:S(2)}) async-start(bf16[2,30,176,512]{3,2,1,0:T(8,128)(2,1)} %bitcast.120), calls=%async_computation.1 | async-start | bytes 21626880 | tf_op jit(solution)/shard_map/all_to_all | solution.py:68
  463.8 524.7 %reduce-scatter.6.cloned.1.call-start = ((), (), s32[]{:S(2)}) async-start(), calls=%async_computation.14 | async-start | bytes 23961600 | tf_op jit(solution)/shard_map/reduce_scatter | solution.py:87
  736.5 491.5 %reduce-scatter.8.cloned.1.call-start = ((), (), s32[]{:S(2)}) async-start(), calls=%async_computation.15 | async-start | bytes 23961600 | tf_op jit(solution)/shard_map/reduce_scatter | solution.py:89
  756.4 720.5 %reduce-scatter.10.cloned.1.call-start = ((), (), s32[]{:S(2)}) async-start(), calls=%async_computation.16 | async-start | bytes 23961600 | tf_op jit(solution)/shard_map/reduce_scatter | solution.py:88
  773.6 0.8 copy-start.5
  773.6 1.4 copy-start.9
  962.7 17.1 %copy-start.8 = (bf16[512,1408]{1,0:T(8,128)(2,1)S(1)}, bf16[512,1408]{1,0:T(8,128)(2,1)}, u32[]{:S(2)}) copy-start(bf16[512,1408]{1,0:T(8,128)(2,1)} %all-gather.15.cloned.1.call-done) | copy-start | bytes 4325380
  979.9 497.0 %copy-start.6 = (f32[1408,8]{0,1:T(8,128)S(1)}, f32[1408,8]{0,1:T(8,128)}, u32[]{:S(2)}) copy-start(f32[1408,8]{0,1:T(8,128)} %get-tuple-element.63) | copy-start | bytes 135172
Sparse Core Ops, SparseCore 0:
  10.7 65.5 all-gather.16
  79.1 61.8 all-gather.14
  143.7 61.8 all-gather.12
  234.9 167.5 all-reduce.10
  405.1 94.9 all-gather.10
  502.6 93.0 all-gather.6
  598.4 93.0 all-gather.8
  694.7 24.5 all-reduce.12
  736.6 242.5 reduce-scatter.5
  984.5 243.4 reduce-scatter.7
  1233.5 243.4 reduce-scatter.9
where the time goes:
time: 1500 us; the launch traced here: 1480 us
  waiting for transfers between devices  862 us (57%)
  local copies, waits for them, and re-layouts  284 us (19%)
  matrix products  232 us (15%)
  other arithmetic  51.5 us (3%)
  starting transfers between devices  22.3 us (1%)
  blocking collectives  18.3 us (1%)
  between operations  15.3 us (1%)
    reduce_scatter x1, waiting for transfers between devices, device_step(): lax.psum_scatter(dw_three, 'fsdp', scatter_dimension=1, tiled=True)  249 us
    reduce_scatter x1, waiting for transfers between devices, device_step(): dw_two = lax.psum_scatter(dw_two, 'fsdp', scatter_dimension=2, tiled=True)  240 us
    all_gather x1, waiting for transfers between devices, device_step(): w_three_full = lax.all_gather(w_three, 'fsdp', axis=1, tiled=True)  80.4 us
    all_gather x1, waiting for transfers between devices, device_step(): w_two_full = lax.all_gather(w_two, 'fsdp', axis=2, tiled=True)  80.4 us
    all_gather x1, waiting for transfers between devices, device_step(): ws_one_full = lax.all_gather(ws_one, 'fsdp', axis=0, tiled=True)  66.9 us
    all_gather x1, waiting for transfers between devices, device_step(): ws_three_full = lax.all_gather(ws_three, 'fsdp', axis=0, tiled=True)  54.9 us
    gather x1, local copies, waits for them, and re-layouts, device_step(): jnp.concatenate([gate_loc.reshape(-1), zero_one])[filled]  54.6 us
    all_gather x1, waiting for transfers between devices, device_step(): ws_two_full = lax.all_gather(ws_two, 'fsdp', axis=1, tiled=True)  46.5 us
  transfers between devices with their start and end apart: 14, of which 9 were waited for; matrix products, arithmetic and copies ran while one was open for 36% of the time, Pallas kernels for 0%

commit v1 on v0

v1 whole, which is shorter than its diff:
```python
import jax
import jax.numpy as jnp
from jax import lax
from jax.sharding import Mesh
from jax.sharding import PartitionSpec as P

CAP_NUM = 5
CAP_DEN = 4
RING = 4


def capacity_for(tok_dev, top_k, n_exp):
    needed = -(-(tok_dev * top_k * CAP_NUM) // (CAP_DEN * n_exp))
    return max(8, -(-needed // 8) * 8)


def route(ids, n_exp, capacity):
    flat = ids.reshape(-1)
    n_assign = flat.shape[0]
    onehot = (flat[:, None] == jnp.arange(n_exp, dtype=jnp.int32)[None, :]).astype(jnp.int32)
    pos = jnp.sum(jnp.cumsum(onehot, axis=0) * onehot, axis=1) - 1
    kept = pos < capacity
    slot = jnp.where(kept, flat * capacity + pos, n_exp * capacity)
    filled = jnp.full((n_exp * capacity + 1,), n_assign, jnp.int32)
    filled = filled.at[slot].set(jnp.arange(n_assign, dtype=jnp.int32))
    return pos, kept, filled[: n_exp * capacity]


def swiglu_backward(x, dy, g, wa, wc, wbt, b):
    f32 = jnp.float32
    up = b + "td," + b + "df->" + b + "tf"
    back = b + "tf," + b + "df->" + b + "td"
    outer = b + "td," + b + "tf->" + b + "df"
    h1 = jnp.einsum(up, x, wa, preferred_element_type=f32)
    h3 = jnp.einsum(up, x, wc, preferred_element_type=f32)
    sig = jax.nn.sigmoid(h1)
    silu = h1 * sig
    a = (silu * h3).astype(jnp.bfloat16)
    da = jnp.einsum(up, g, wbt, preferred_element_type=f32)
    dh1 = (da * h3 * sig * (1.0 + h1 * (1.0 - sig))).astype(jnp.bfloat16)
    dh3 = (da * silu).astype(jnp.bfloat16)
    dx = (jnp.einsum(back, dh1, wa, preferred_element_type=f32) + jnp.einsum(back, dh3, wc, preferred_element_type=f32)).astype(jnp.bfloat16)
    dwa = jnp.einsum(outer, x, dh1, preferred_element_type=f32)
    dwc = jnp.einsum(outer, x, dh3, preferred_element_type=f32)
    dwbt = jnp.einsum(outer, g, a, preferred_element_type=f32)
    if dy is None:
        return dx, None, dwa, dwc, dwbt
    y = jnp.einsum(back, a, wbt, preferred_element_type=f32)
    dgate = jnp.sum(dy.astype(f32) * y, axis=-1)
    return dx, dgate, dwa, dwc, dwbt


def solution(mesh):
    n_fsdp, n_core = mesh.devices.shape
    plane = n_fsdp // RING
    mesh4 = Mesh(mesh.devices.reshape(RING, plane, n_core), ("z", "p", "core"))
    tok = P(("z", "p", "core"), None)
    in_specs = (tok, tok, tok, tok, P("core", ("z", "p"), None), P("core", None, ("z", "p")), P("core", ("z", "p"), None), P(("z", "p"), None), P(None, ("z", "p")), P(("z", "p"), None))
    out_specs = (tok, tok, P("core", ("z", "p"), None), P("core", None, ("z", "p")), P("core", ("z", "p"), None), P(("z", "p"), None), P(None, ("z", "p")), P(("z", "p"), None))

    def device_step(x, dy, ids, gate, w1, w2, w3, ws1, ws2, ws3):
        t, k = ids.shape
        d = x.shape[1]
        nl, dl, ff = w1.shape
        n_exp = nl * n_core
        cap = capacity_for(t, k, n_exp)
        eo = -(-nl // RING)
        nb = RING * n_core
        zi = lax.axis_index("z")
        ci = lax.axis_index("core")
        fsh = ws1.shape[1]

        wss = jnp.stack([ws1, ws3, ws2.T])
        wsg = lax.all_gather(wss, ("z", "p"), axis=1, tiled=True)
        wst = jnp.stack([w1, w3, w2.transpose(0, 2, 1)])
        wst = jnp.pad(wst, ((0, 0), (0, RING * eo - nl), (0, 0), (0, 0))).reshape(3, RING, eo, dl, ff)
        wz = lax.all_to_all(wst.transpose(1, 0, 2, 3, 4), "z", 0, 0, tiled=True)
        wz = wz.transpose(1, 2, 0, 3, 4)
        wg = lax.all_gather(wz, "p", axis=3, tiled=True).reshape(3, eo, d, ff)

        fwd = [(i, (i + 1) % RING) for i in range(RING)]
        bwd = [(i, (i - 1) % RING) for i in range(RING)]
        half = t // 2
        xs, dys = [], []
        for src, acc in ((x, xs), (dy, dys)):
            m1 = lax.ppermute(src, "z", bwd)
            p1 = lax.ppermute(src, "z", fwd)
            p2 = lax.ppermute(p1[:half], "z", fwd)
            m2 = lax.ppermute(m1[half:], "z", bwd)
            blocks = [src, m1, jnp.concatenate([p2, m2]), p1]
            for blk in blocks:
                acc.append(blk)
                acc.append(lax.ppermute(blk, "core", [(i, (i + 1) % n_core) for i in range(n_core)]))

        pos, kept, filled = route(ids, n_exp, cap)
        tokf = jnp.where(filled < t * k, filled // k, t).astype(jnp.float32)
        gatef = jnp.concatenate([gate.reshape(-1), jnp.zeros((1,), jnp.float32)])[filled]
        meta = jnp.stack([tokf, gatef]).reshape(2, n_core, nl, cap)
        meta = jnp.pad(meta, ((0, 0), (0, 0), (0, RING * eo - nl), (0, 0)), constant_values=float(0))
        meta = meta.reshape(2, n_core, RING, eo, cap).transpose(2, 1, 0, 3, 4).reshape(nb, 2, eo, cap)
        meta = lax.all_to_all(meta, ("z", "core"), 0, 0, tiled=True)
        rel = jnp.arange(nb, dtype=jnp.int32)
        order = ((zi + rel // n_core) % RING) * n_core + (ci + rel % n_core) % n_core
        meta = meta[order]
        tok_idx = meta[:, 0].astype(jnp.int32)
        gates = meta[:, 1].transpose(1, 0, 2).reshape(eo, nb * cap)

        xg = jnp.stack([xs[b].at[tok_idx[b]].get(mode="fill", fill_value=0) for b in range(nb)], axis=1).reshape(eo, nb * cap, d)
        dyg = jnp.stack([dys[b].at[tok_idx[b]].get(mode="fill", fill_value=0) for b in range(nb)], axis=1).reshape(eo, nb * cap, d)
        gg = (gates[..., None] * dyg.astype(jnp.float32)).astype(jnp.bfloat16)
        dxr, dgr, dwa, dwc, dwbt = swiglu_backward(xg, dyg, gg, wg[0], wg[1], wg[2], "e")

        dxr = dxr.reshape(eo, nb, cap, d)
        back = []
        for b in range(nb):
            kz, kc = b // n_core, b % n_core
            perm = [(z * n_core + c, ((z + kz) % RING) * n_core + (c + kc) % n_core) for z in range(RING) for c in range(n_core)]
            blk = dxr[:, b]
            back.append(blk if b == 0 else lax.ppermute(blk, ("z", "core"), perm))
        dx_back = jnp.concatenate([jnp.stack(back).reshape(nb * eo * cap, d), jnp.zeros((1, d), jnp.bfloat16)])
        dgr = dgr.reshape(eo, nb, cap).transpose(1, 0, 2)
        inv = ((rel // n_core - zi) % RING) * n_core + (rel % n_core + ci) % n_core
        dg_back = lax.all_to_all(dgr[inv], ("z", "core"), 0, 0, tiled=True).reshape(-1)

        flat = ids.reshape(-1)
        co, lo = flat // nl, flat % nl
        zo, io = lo // eo, lo % eo
        mrel = ((zi - zo) % RING) * n_core + (ci + co) % n_core
        slot = jnp.where(kept, (mrel * eo + io) * cap + pos, nb * eo * cap)
        slot_abs = jnp.where(kept, ((zo * n_core + co) * eo + io) * cap + pos, nb * eo * cap)
        dx_assign = dx_back[slot].reshape(t, k, d)
        dgate = jnp.concatenate([dg_back, jnp.zeros((1,), jnp.float32)])[slot_abs].reshape(t, k)

        dxs, _, dsa, dsc, dsbt = swiglu_backward(x, None, dy, wsg[0], wsg[1], wsg[2], "")
        dx = (jnp.sum(dx_assign.astype(jnp.float32), axis=1) + dxs.astype(jnp.float32)).astype(jnp.bfloat16)

        span = -(-fsh // (128 * n_core)) * 128
        off = fsh - span
        ds = jnp.stack([dsa, dsc, dsbt])
        mine = lax.dynamic_slice_in_dim(ds, ci * off, span, axis=2)
        other = lax.dynamic_slice_in_dim(ds, (1 - ci) * off, span, axis=2)
        mine = mine + lax.ppermute(other, "core", [(0, 1), (1, 0)])
        mine = lax.psum_scatter(mine, ("z", "p"), scatter_dimension=1, tiled=True)
        both = lax.all_gather(mine, "core")
        dsg = jnp.concatenate([both[0][..., :off], both[1]], axis=-1)

        def reduce(dw):
            return lax.psum_scatter(dw.reshape(eo, RING, d // RING, ff), "p", scatter_dimension=2, tiled=True)

        dws = jnp.stack([reduce(dwa), reduce(dwc), reduce(dwbt)])
        dws = lax.all_to_all(dws.transpose(2, 0, 1, 3, 4), "z", 0, 0, tiled=True)
        dws = dws.transpose(1, 0, 2, 3, 4).reshape(3, RING * eo, dl, ff)[:, :nl]
        return dx, dgate, dws[0], dws[2].transpose(0, 2, 1), dws[1], dsg[0], dsg[2].T, dsg[1]

    return jax.shard_map(device_step, mesh=mesh4, in_specs=in_specs, out_specs=out_specs, check_vma=False)
```

time: 1500 us -> 974 us (0.65)
  waiting for transfers between devices: 862 us -> 78.1 us
  local copies, waits for them, and re-layouts: 284 us -> 500 us
  other arithmetic: 51.5 us -> 117 us
  matrix products: 232 us -> 202 us
  starting transfers between devices: 22.3 us -> 40.9 us
  blocking collectives: 18.3 us -> 2.02 us
    reduce_scatter x3, waiting for transfers between devices: 488 us -> 0.01 us  [reduce(): lax.psum_scatter(dw.reshape(eo, RING, d // RING, ff), 'p', scatter_dimens...]
    all_gather x6 -> x2, waiting for transfers between devices: 365 us -> 0.02 us  [the longest x1 0.02 us: device_step(): wg = lax.all_gather(wz, 'p', axis=3, tiled=True).reshape(3, eo, d, ff)]
    gather x5 -> x21, local copies, waits for them, and re-layouts: 203 us -> 255 us  [the longest x16 114 us: device_step(): xs[b].at[tok_idx[b]].get(mode='fill', fill_value=0)]
    ppermute x0 -> x24, waiting for transfers between devices: none -> 50.1 us  [the longest x7 50.1 us: device_step(): back.append(blk if b == 0 else lax.ppermute(blk, ('z', 'core'), perm))]
    reshape x4 -> x12, local copies, waits for them, and re-layouts: 2.54 us -> 49.6 us  [the longest x6 47.1 us: reduce(): dw.reshape(eo, RING, d // RING, ff)]
    slice x1 -> x12, local copies, waits for them, and re-layouts: 1.62 us -> 34.7 us  [the longest x2 12.4 us: device_step(): wg[1]]
    dot_general x17, matrix products: 232 us -> 202 us  [the longest x2 34.8 us: swiglu_backward(): h3 = jnp.einsum(up, x, wc, preferred_element_type=f32)]
    convert_element_type x1 -> x4, other arithmetic: 1.51 us -> 26.7 us  [the longest x2 25.1 us: device_step(): gg = (gates[..., None] * dyg.astype(jnp.float32)).astype(jnp.bfloat16)]
  transfers between devices with their start and end apart: 14 -> 34, of which waited for: 9 -> 6; matrix products, arithmetic and copies ran while one was open for 36% -> 85% of each run, Pallas kernels for 0% -> 0%
where the time goes in v1:
time: 974 us; the launch traced here: 956 us
  local copies, waits for them, and re-layouts  500 us (51%)
  matrix products  202 us (21%)
  other arithmetic  117 us (12%)
  waiting for transfers between devices  78.1 us (8%)
  starting transfers between devices  40.9 us (4%)
  between operations  16 us (2%)
    gather x16, local copies, waits for them, and re-layouts, device_step(): xs[b].at[tok_idx[b]].get(mode='fill', fill_value=0)  114 us
    gather x1, local copies, waits for them, and re-layouts, device_step(): jnp.concatenate([gate.reshape(-1), jnp.zeros((1,), jnp.float32)])[filled]  54.6 us
    ppermute x7, waiting for transfers between devices, device_step(): back.append(blk if b == 0 else lax.ppermute(blk, ('z', 'core'), perm))  50.1 us
    reshape x6, local copies, waits for them, and re-layouts, reduce(): dw.reshape(eo, RING, d // RING, ff)  47.1 us
    gather x1, local copies, waits for them, and re-layouts, device_step(): jnp.concatenate([dg_back, jnp.zeros((1,), jnp.float32)])[slot_abs]  45.5 us
    gather x1, local copies, waits for them, and re-layouts, device_step(): dx_assign = dx_back[slot].reshape(t, k, d)  39.6 us
    another operation x3, other arithmetic  37.1 us
    dot_general x2, matrix products, swiglu_backward(): h3 = jnp.einsum(up, x, wc, preferred_element_type=f32)  34.8 us
  transfers between devices with their start and end apart: 34, of which 6 were waited for; matrix products, arithmetic and copies ran while one was open for 85% of the time, Pallas kernels for 0%

profile of v1, /device:TPU:1, one launch (start us, length us, event | category | flops | bytes accessed | tf_op | source)
XLA Modules:
  0.0 956.3 jit_solution(12078821742573598496)
XLA Ops:
  20.6 34.1 %reduce-window.6 = s32[60,64,128]{2,1,0:T(8,128)} reduce-window(s32[60,64,128]{2,1,0:T(8,128)} %fusion.16, s32[]{:T(128)} %constant.153.clone.1), window={size=1x1x128 pad=0_0x0_0x127_0}, to_apply=%region_0.1 | reduce-window | flops 62423040 | bytes 3932164 | tf_op jit(solution)/shard_map/reduce-window
  72.4 30.8 %scatter_custom_fusion = s32[10561]{0:T(1024)S(1)} fusion(s32[8192]{0:T(1024)S(1)} %bitcast.378, s32[8192]{0:T(1024)S(1)} %iota.20, s32[]{:T(128)} %constant.152.clone.1), kind=kCustom, calls=%fused_computation.181 | custom fusion | bytes 42248 | tf_op jit(solution)/shard_map/scatter | solution.py:25
  104.3 54.6 %gather_fusion = f32[10560]{0:T(1024)S(1)} fusion(f32[8193]{0:T(1024)S(1)} %pad_maximum_fusion.4, s32[11264]{0:T(1024)S(1)} %pad_clamp_fusion), kind=kCustom, calls=%fused_computation | custom fusion | bytes 126720 | tf_op jit(solution)/shard_map/gather | solution.py:97
  174.5 8.5 all-to-all-done.1
  269.9 9.6 %fusion.19 = f32[1408,2048]{1,0:T(8,128)} fusion(bf16[2048,512]{1,0:T(8,128)(2,1)} %param.10, bf16[3,512,1408]{2,1,0:T(8,128)(2,1)} %all-gather.6.cloned.1.call-done), kind=kOutput, calls=%fused_computation.96 | convolution fusion | flops 2952790016 | bytes 15073280 | tf_op jit(solution)/shard_map/td,df->tf/dot_general | solution.py:35
  287.1 14.5 %fusion.9 = (bf16[2048,1408]{0,1:T(8,128)(2,1)}, bf16[2048,1408]{0,1:T(8,128)(2,1)}) fusion(f32[1408,2048]{1,0:T(8,128)} %fusion.21, f32[1408,2048]{1,0:T(8,128)} %fusion.19, bf16[2048,512]{1,0:T(8,128)(2,1)S(1)} %copy-done, bf16[3,512,1408]{2,1,0:T(8,128)(2,1)} %all-gather.6.cloned.1.call-done), kind=kOutput, calls=%fused_computation.45 | convolution fusion | flops 2990276608 | bytes 38141952 | tf_op jit(solution)/shard_map/td,df->tf/dot_general | solution.py:39
  301.6 9.6 %fusion.12 = f32[1,512,1408]{1,2,0:T(8,128)S(1)} fusion(bf16[2048,512]{1,0:T(8,128)(2,1)S(1)} %copy-done, f32[1408,2048]{1,0:T(8,128)} %fusion.19, f32[1408,2048]{1,0:T(8,128)} %fusion.21), kind=kOutput, calls=%fused_computation.51 | convolution fusion | flops 2970091520 | bytes 28049408 | tf_op jit(solution)/shard_map/td,tf->df/dot_general | solution.py:45
  402.0 11.5 %multiply_convert_fusion = bf16[8,1408,512]{2,1,0:T(8,128)(2,1)} fusion(f32[8,1408]{1,0:T(8,128)S(1)} %copy-done.17, bf16[8,8,176,512]{3,2,1,0:T(8,128)(2,1)} %get-tuple-element.105), kind=kLoop, calls=%fused_computation.24 | loop fusion | flops 17301504 | bytes 23113728 | tf_op jit(solution)/shard_map/convert_element_type | solution.py:110
  466.2 11.6 %fusion.56 = f32[8,1408,352]{1,2,0:T(8,128)} fusion(bf16[8,1408,512]{2,1,0:T(8,128)(2,1)} %multiply_convert_fusion, bf16[8,512,352]{1,2,0:T(8,128)(2,1)} %squeeze.132), kind=kOutput, calls=%fused_computation.239 | convolution fusion | flops 4060086272 | bytes 30277632 | tf_op jit(solution)/shard_map/etd,edf->etf/dot_general | solution.py:39
  477.8 10.6 %fusion.57 = f32[8,1408,352]{1,2,0:T(8,128)} fusion(bf16[8,1408,512]{2,1,0:T(8,128)(2,1)} %bitcast.65, bf16[8,512,352]{1,2,0:T(8,128)(2,1)S(1)} %squeeze.134), kind=kOutput, calls=%fused_computation.240 | convolution fusion | flops 4060086272 | bytes 30277632 | tf_op jit(solution)/shard_map/etd,edf->etf/dot_general | solution.py:34
  488.5 25.3 %multiply_convert_fusion.1 = (bf16[8,1408,352]{1,2,0:T(8,128)(2,1)}, bf16[8,1408,352]{1,2,0:T(8,128)(2,1)}, bf16[8,1408,352]{1,2,0:T(8,128)(2,1)}) fusion(f32[8,1408,352]{1,2,0:T(8,128)} %fusion.57, f32[8,1408,352]{1,2,0:T(8,128)} %fusion.56, bf16[8,1408,512]{2,1,0:T(8,128)(2,1)} %bitcast.65, bf16[8,512,352]{1,2,0:T(8,128)(2,1)} %squeeze.133), kind=kOutput, calls=%fused_computation.25 | convolution fusion | flops 4119560192 | bytes 69926912 | tf_op jit(solution)/shard_map/etd,edf->etf/dot_general | solution.py:35
  513.7 13.8 %fusion.61 = f32[8,512,352]{1,2,0:T(8,128)} fusion(bf16[8,1408,352]{1,2,0:T(8,128)(2,1)} %get-tuple-element.59, bf16[8,1408,512]{2,1,0:T(8,128)(2,1)} %multiply_convert_fusion), kind=kOutput, calls=%fused_computation.244 | convolution fusion | flops 4060086272 | bytes 25231360 | tf_op jit(solution)/shard_map/etd,etf->edf/dot_general | solution.py:45
  534.9 8.2 copy.267
  543.1 13.8 %fusion.59 = f32[8,512,352]{1,2,0:T(8,128)} fusion(bf16[8,1408,352]{1,2,0:T(8,128)(2,1)} %get-tuple-element.60, bf16[8,1408,512]{2,1,0:T(8,128)(2,1)} %bitcast.65), kind=kOutput, calls=%fused_computation.242 | convolution fusion | flops 4060086272 | bytes 25231360 | tf_op jit(solution)/shard_map/etd,etf->edf/dot_general | solution.py:43
  564.4 8.2 copy.265
  574.5 13.7 %fusion.60 = f32[8,512,352]{1,2,0:T(8,128)} fusion(bf16[8,1408,352]{1,2,0:T(8,128)(2,1)} %get-tuple-element.61, bf16[8,1408,512]{2,1,0:T(8,128)(2,1)} %bitcast.65), kind=kOutput, calls=%fused_computation.243 | convolution fusion | flops 4060086272 | bytes 25231360 | tf_op jit(solution)/shard_map/etd,etf->edf/dot_general | solution.py:44
  595.8 8.3 copy.266
  604.1 13.6 %bitcast_convert_fusion = f32[8,1408,512]{2,1,0:T(8,128)} fusion(bf16[8,8,176,512]{3,2,1,0:T(8,128)(2,1)} %get-tuple-element.105), kind=kLoop, calls=%fused_computation.30 | loop fusion | flops 5767168 | bytes 34603008 | tf_op jit(solution)/shard_map/convert_element_type | solution.py:110
  617.7 23.3 %copy.263 = f32[8,1408,512]{1,2,0:T(8,128)} copy(f32[8,1408,512]{2,1,0:T(8,128)} %bitcast_convert_fusion) | data formatting | bytes 46137344 | tf_op jit(solution)/shard_map/convert_element_type | solution.py:110
  641.0 8.5 fusion.20
  649.5 14.8 %fusion.58 = f32[8,1408,512]{2,1,0:T(8,128)} fusion(bf16[8,1408,352]{1,2,0:T(8,128)(2,1)} %get-tuple-element.60, bf16[8,512,352]{1,2,0:T(8,128)(2,1)S(1)} %squeeze.134), kind=kOutput, calls=%fused_computation.241 | convolution fusion | flops 4060086272 | bytes 33882112 | tf_op jit(solution)/shard_map/etf,edf->etd/dot_general | solution.py:42
  664.3 18.2 %add_convert_fusion = bf16[8,1408,512]{2,1,0:T(8,128)(2,1)} fusion(f32[8,1408,512]{2,1,0:T(8,128)} %fusion.58, bf16[8,1408,352]{1,2,0:T(8,128)(2,1)} %get-tuple-element.61, bf16[8,512,352]{1,2,0:T(8,128)(2,1)} %squeeze.133), kind=kOutput, calls=%fused_computation.23 | convolution fusion | flops 4071620608 | bytes 45416448 | tf_op jit(solution)/shard_map/etf,edf->etd/dot_general | solution.py:42
  690.7 13.4 %multiply_reduce_fusion = f32[8,1408]{1,0:T(8,128)S(1)} fusion(f32[8,1408,512]{1,2,0:T(8,128)} %copy.263, bf16[8,1408,352]{1,2,0:T(8,128)(2,1)} %get-tuple-element.59, bf16[8,512,352]{1,2,0:T(8,128)(2,1)S(1)} %copy-done.2), kind=kOutput, calls=%fused_computation.22 | convolution fusion | flops 4071609344 | bytes 33927168 | tf_op jit(solution)/shard_map/etf,edf->etd/dot_general | solution.py:48
  717.6 9.1 all-to-all-done.2
  726.9 45.5 %gather_fusion.20 = f32[8192]{0:T(1024)S(1)} fusion(f32[11265]{0:T(1024)S(1)} %pad_maximum_fusion.2, s32[8192]{0:T(1024)S(1)} %broadcast_clamp_fusion), kind=kCustom, calls=%fused_computation.20 | custom fusion | bytes 98304 | tf_op jit(solution)/shard_map/gather | solution.py:132
  784.7 33.6 %collective-permute-done.18 = bf16[8,176,512]{2,1,0:T(8,128)(2,1)} collective-permute-done((bf16[8,176,512]{2,1,0:T(8,128)(2,1)}, bf16[8,176,512]{2,1,0:T(8,128)(2,1)}, u32[]{:S(2)}, u32[]{:S(2)}) %collective-permute-start.18) | collective-permute-done | bytes 1441824 | tf_op jit(solution)/shard_map/ppermute | solution.py:119
  826.0 16.4 %collective-permute-done.22 = bf16[8,176,512]{2,1,0:T(8,128)(2,1)S(1)} collective-permute-done((bf16[8,176,512]{2,1,0:T(8,128)(2,1)S(1)}, bf16[8,176,512]{2,1,0:T(8,128)(2,1)S(1)}, u32[]{:S(2)}, u32[]{:S(2)}) %collective-permute-start.22) | collective-permute-done | bytes 1441824 | tf_op jit(solution)/shard_map/ppermute | solution.py:119
  843.6 10.1 %concatenate.22 = bf16[11265,512]{1,0:T(8,128)(2,1)} pad(bf16[11264,512]{1,0:T(8,128)(2,1)} %bitcast.344, bf16[]{:T(256)} %constant.171.clone.1), padding=0_1x0_0 | pad | bytes 23069698 | tf_op jit(solution)/shard_map/concatenate | solution.py:120
  853.7 39.6 %gather_fusion.18 = bf16[8192,512]{1,0:T(8,128)(2,1)} fusion(bf16[11265,512]{1,0:T(8,128)(2,1)} %concatenate.22, s32[8192]{0:T(1024)S(1)} %broadcast_clamp_fusion.1), kind=kCustom, calls=%fused_computation.18 | custom fusion | bytes 16809984 | tf_op jit(solution)/shard_map/gather | solution.py:131
  893.3 15.5 %reshape.1081 = f32[2048,4,512]{2,1,0:T(4,128)} reshape(bf16[8192,512]{1,0:T(8,128)(2,1)} %gather_fusion.18) | data formatting | bytes 25165824 | tf_op jit(solution)/shard_map/convert_element_type | solution.py:135
  908.8 16.1 %reduce_sum.28 = f32[2048,512]{1,0:T(8,128)} reduce(f32[2048,4,512]{2,1,0:T(4,128)} %reshape.1081, f32[]{:T(128)} %constant.164.clone.1), dimensions={1}, to_apply=%region_4.5 | reduce | flops 3145728 | bytes 20971524 | tf_op jit(solution)/shard_map/reduce_sum | solution.py:135
  931.4 10.3 %add_convert_fusion.1 = bf16[2048,512]{1,0:T(8,128)(2,1)} fusion(f32[2048,512]{1,0:T(8,128)} %reduce_sum.28, f32[2048,512]{1,0:T(8,128)} %fusion.20, bf16[2048,1408]{0,1:T(8,128)(2,1)} %get-tuple-element.62, bf16[3,512,1408]{2,1,0:T(8,128)(2,1)} %all-gather.6.cloned.1.call-done), kind=kOutput, calls=%fused_computation.49 | convolution fusion | flops 2958032896 | bytes 17694720 | tf_op jit(solution)/shard_map/tf,df->td/dot_general | solution.py:42
  (267 shorter events, 365.7 us)
Async XLA Ops:
  7.2 262.7 %all-gather.6.cloned.1.call-start = ((), (), s32[]{:S(2)}) async-start(), calls=%async_computation.8 | async-start | bytes 4392960 | tf_op jit(solution)/shard_map/all_gather | solution.py:74
  8.6 186.9 %collective-permute-start = (bf16[2048,512]{1,0:T(8,128)(2,1)}, bf16[2048,512]{1,0:T(8,128)(2,1)}, u32[]{:S(2)}, u32[]{:S(2)}) collective-permute-start(bf16[2048,512]{1,0:T(8,128)(2,1)} %param.11), channel_id=1, source_target_pairs={{0,1},{1,0},{2,3},{3,2},{4,5},{5,4},{6,7},{7,6},{8,9},{9,8},{10,11... | collective-permute-start | bytes 6291464 | tf_op jit(solution)/shard_map/ppermute | solution.py:93
  10.1 178.2 %collective-permute-start.1 = (bf16[2048,512]{1,0:T(8,128)(2,1)}, bf16[2048,512]{1,0:T(8,128)(2,1)}, u32[]{:S(2)}, u32[]{:S(2)}) collective-permute-start(bf16[2048,512]{1,0:T(8,128)(2,1)} %param.11), channel_id=1, source_target_pairs={{0,96},{32,0},{64,32},{96,64},{1,97},{33,1},{65,33},{97,65},{2,98}... | collective-permute-start | bytes 6291464 | tf_op jit(solution)/shard_map/ppermute | solution.py:86
  14.0 152.3 %collective-permute-start.3 = (bf16[2048,512]{1,0:T(8,128)(2,1)}, bf16[2048,512]{1,0:T(8,128)(2,1)S(1)}, u32[]{:S(2)}, u32[]{:S(2)}) collective-permute-start(bf16[2048,512]{1,0:T(8,128)(2,1)} %param.11), channel_id=1, source_target_pairs={{0,32},{32,64},{64,96},{96,0},{1,33},{33,65},{65,97},{97,1},{2,34}... | collective-permute-start | bytes 6291464 | tf_op jit(solution)/shard_map/ppermute | solution.py:87
  14.0 176.6 %collective-permute-start.9 = (bf16[2048,512]{1,0:T(8,128)(2,1)}, bf16[2048,512]{1,0:T(8,128)(2,1)}, u32[]{:S(2)}, u32[]{:S(2)}) collective-permute-start(bf16[2048,512]{1,0:T(8,128)(2,1)} %param.10), channel_id=1, source_target_pairs={{0,96},{32,0},{64,32},{96,64},{1,97},{33,1},{65,33},{97,65},{2,98}... | collective-permute-start | bytes 6291464 | tf_op jit(solution)/shard_map/ppermute | solution.py:86
  16.7 169.1 %collective-permute-start.11 = (bf16[2048,512]{1,0:T(8,128)(2,1)}, bf16[2048,512]{1,0:T(8,128)(2,1)}, u32[]{:S(2)}, u32[]{:S(2)}) collective-permute-start(bf16[2048,512]{1,0:T(8,128)(2,1)} %param.10), channel_id=1, source_target_pairs={{0,32},{32,64},{64,96},{96,0},{1,33},{33,65},{65,97},{97,1},{2,34}... | collective-permute-start | bytes 6291464 | tf_op jit(solution)/shard_map/ppermute | solution.py:87
  166.2 84.4 %collective-permute-start.8 = (bf16[2048,512]{1,0:T(8,128)(2,1)}, bf16[2048,512]{1,0:T(8,128)(2,1)}, u32[]{:S(2)}, u32[]{:S(2)}) collective-permute-start(bf16[2048,512]{1,0:T(8,128)(2,1)} %param.10), channel_id=1, source_target_pairs={{0,1},{1,0},{2,3},{3,2},{4,5},{5,4},{6,7},{7,6},{8,9},{9,8},{10,11... | collective-permute-start | bytes 6291464 | tf_op jit(solution)/shard_map/ppermute | solution.py:93
  173.8 252.8 %all-gather.4.cloned.1.call-start = ((), (), s32[]{:S(2)}) async-start(), calls=%async_computation.7 | async-start | bytes 10027008 | tf_op jit(solution)/shard_map/all_gather | solution.py:79
  183.9 590.6 %all-reduce.6.cloned.1.call-start = ((), (), s32[]{:S(2)}) async-start(), calls=%async_computation.12 | async-start | bytes 12582912
  185.8 75.2 %collective-permute-start.4 = (bf16[1024,512]{1,0:T(8,128)(2,1)}, bf16[1024,512]{1,0:T(8,128)(2,1)}, u32[]{:S(2)}, u32[]{:S(2)}) collective-permute-start(bf16[1024,512]{1,0:T(8,128)(2,1)} %slice.241), channel_id=1, source_target_pairs={{0,32},{32,64},{64,96},{96,0},{1,33},{33,65},{65,97},{97,1},{2,34}... | collective-permute-start | bytes 3145736 | tf_op jit(solution)/shard_map/ppermute | solution.py:88
  188.3 74.9 %collective-permute-start.12 = (bf16[1024,512]{1,0:T(8,128)(2,1)}, bf16[1024,512]{1,0:T(8,128)(2,1)}, u32[]{:S(2)}, u32[]{:S(2)}) collective-permute-start(bf16[1024,512]{1,0:T(8,128)(2,1)} %slice.247), channel_id=1, source_target_pairs={{0,32},{32,64},{64,96},{96,0},{1,33},{33,65},{65,97},{97,1},{2,34}... | collective-permute-start | bytes 3145736 | tf_op jit(solution)/shard_map/ppermute | solution.py:88
  190.6 75.5 %collective-permute-start.5 = (bf16[1024,512]{1,0:T(8,128)(2,1)}, bf16[1024,512]{1,0:T(8,128)(2,1)}, u32[]{:S(2)}, u32[]{:S(2)}) collective-permute-start(bf16[1024,512]{1,0:T(8,128)(2,1)} %slice.242), channel_id=1, source_target_pairs={{0,96},{32,0},{64,32},{96,64},{1,97},{33,1},{65,33},{97,65},{2,98}... | collective-permute-start | bytes 3145736 | tf_op jit(solution)/shard_map/ppermute | solution.py:89
  195.6 72.8 %collective-permute-start.13 = (bf16[1024,512]{1,0:T(8,128)(2,1)}, bf16[1024,512]{1,0:T(8,128)(2,1)S(1)}, u32[]{:S(2)}, u32[]{:S(2)}) collective-permute-start(bf16[1024,512]{1,0:T(8,128)(2,1)} %slice.248), channel_id=1, source_target_pairs={{0,96},{32,0},{64,32},{96,64},{1,97},{33,1},{65,33},{97,65},{2,98}... | collective-permute-start | bytes 3145736 | tf_op jit(solution)/shard_map/ppermute | solution.py:89
  250.6 67.2 %collective-permute-start.2 = (bf16[2048,512]{1,0:T(8,128)(2,1)}, bf16[2048,512]{1,0:T(8,128)(2,1)}, u32[]{:S(2)}, u32[]{:S(2)}) collective-permute-start(bf16[2048,512]{1,0:T(8,128)(2,1)} %collective-permute-done.1), channel_id=1, source_target_pairs={{0,1},{1,0},{2,3},{3,2},{4,5},{5,4},{6,7},{7,6},{8,9},{9,8},{10,11... | collective-permute-start | bytes 6291464 | tf_op jit(solution)/shard_map/ppermute | solution.py:93
  261.0 63.6 %collective-permute-start.10 = (bf16[2048,512]{1,0:T(8,128)(2,1)}, bf16[2048,512]{1,0:T(8,128)(2,1)}, u32[]{:S(2)}, u32[]{:S(2)}) collective-permute-start(bf16[2048,512]{1,0:T(8,128)(2,1)} %collective-permute-done.9), channel_id=1, source_target_pairs={{0,1},{1,0},{2,3},{3,2},{4,5},{5,4},{6,7},{7,6},{8,9},{9,8},{10,11... | collective-permute-start | bytes 6291464 | tf_op jit(solution)/shard_map/ppermute | solution.py:93
  263.2 95.7 %collective-permute-start.7 = (bf16[2048,512]{1,0:T(8,128)(2,1)S(1)}, bf16[2048,512]{1,0:T(8,128)(2,1)}, u32[]{:S(2)}, u32[]{:S(2)}) collective-permute-start(bf16[2048,512]{1,0:T(8,128)(2,1)S(1)} %collective-permute-done.3), channel_id=1, source_target_pairs={{0,1},{1,0},{2,3},{3,2},{4,5},{5,4},{6,7},{7,6},{8,9},{9,8},{10,11... | collective-permute-start | bytes 6291464 | tf_op jit(solution)/shard_map/ppermute | solution.py:93
  266.1 99.8 %collective-permute-start.15 = (bf16[2048,512]{1,0:T(8,128)(2,1)}, bf16[2048,512]{1,0:T(8,128)(2,1)}, u32[]{:S(2)}, u32[]{:S(2)}) collective-permute-start(bf16[2048,512]{1,0:T(8,128)(2,1)} %collective-permute-done.11), channel_id=1, source_target_pairs={{0,1},{1,0},{2,3},{3,2},{4,5},{5,4},{6,7},{7,6},{8,9},{9,8},{10,11... | collective-permute-start | bytes 6291464 | tf_op jit(solution)/shard_map/ppermute | solution.py:93
  268.3 110.7 %collective-permute-start.6 = (bf16[2048,512]{1,0:T(8,128)(2,1)}, bf16[2048,512]{1,0:T(8,128)(2,1)}, u32[]{:S(2)}, u32[]{:S(2)}) collective-permute-start(bf16[2048,512]{1,0:T(8,128)(2,1)} %constant_dynamic-update-slice_fusion), channel_id=1, source_target_pairs={{0,1},{1,0},{2,3},{3,2},{4,5},{5,4},{6,7},{7,6},{8,9},{9,8},{10,11... | collective-permute-start | bytes 6291464 | tf_op jit(solution)/shard_map/ppermute | solution.py:93
  317.8 68.5 %collective-permute-start.14 = (bf16[2048,512]{1,0:T(8,128)(2,1)}, bf16[2048,512]{1,0:T(8,128)(2,1)}, u32[]{:S(2)}, u32[]{:S(2)}) collective-permute-start(bf16[2048,512]{1,0:T(8,128)(2,1)} %constant_dynamic-update-slice_fusion.2), channel_id=1, source_target_pairs={{0,1},{1,0},{2,3},{3,2},{4,5},{5,4},{6,7},{7,6},{8,9},{9,8},{10,11... | collective-permute-start | bytes 6291464 | tf_op jit(solution)/shard_map/ppermute | solution.py:93
  324.6 88.9 %collective-permute-start.23 = (f32[3,512,768]{1,2,0:T(8,128)}, f32[3,512,768]{1,2,0:T(8,128)}, u32[]{:S(2)}, u32[]{:S(2)}) collective-permute-start(f32[3,512,768]{1,2,0:T(8,128)} %constant_dynamic-slice_fusion.1), channel_id=1, source_target_pairs={{0,1},{1,0},{2,3},{3,2},{4,5},{5,4},{6,7},{7,6},{8,9},{9,8},{10,11... | collective-permute-start | bytes 14155784 | tf_op jit(solution)/shard_map/ppermute | solution.py:142
  426.6 498.3 %reduce-scatter.8.cloned.1.call-start = ((), (), s32[]{:S(2)}) async-start(), calls=%async_computation.11 | async-start | bytes 6684672 | tf_op jit(solution)/shard_map/reduce_scatter | solution.py:148
  543.1 381.8 %reduce-scatter.4.cloned.1.call-start = ((), (), s32[]{:S(2)}) async-start(), calls=%async_computation.9 | async-start | bytes 6684672 | tf_op jit(solution)/shard_map/reduce_scatter | solution.py:148
  572.5 352.3 %reduce-scatter.6.cloned.1.call-start = ((), (), s32[]{:S(2)}) async-start(), calls=%async_computation.10 | async-start | bytes 6684672 | tf_op jit(solution)/shard_map/reduce_scatter | solution.py:148
  690.3 87.9 %collective-permute-start.16 = (bf16[8,176,512]{2,1,0:T(8,128)(2,1)}, bf16[8,176,512]{2,1,0:T(8,128)(2,1)}, u32[]{:S(2)}, u32[]{:S(2)}) collective-permute-start(bf16[8,176,512]{2,1,0:T(8,128)(2,1)} %get-tuple-element.69), channel_id=1, source_target_pairs={{0,1},{1,0},{32,33},{33,32},{64,65},{65,64},{96,97},{97,96},{2,3},... | collective-permute-start | bytes 4325384 | tf_op jit(solution)/shard_map/ppermute | solution.py:119
  690.4 90.4 %collective-permute-start.17 = (bf16[8,176,512]{2,1,0:T(8,128)(2,1)}, bf16[8,176,512]{2,1,0:T(8,128)(2,1)}, u32[]{:S(2)}, u32[]{:S(2)}) collective-permute-start(bf16[8,176,512]{2,1,0:T(8,128)(2,1)} %get-tuple-element.68), channel_id=1, source_target_pairs={{0,32},{1,33},{32,64},{33,65},{64,96},{65,97},{96,0},{97,1},{2,34}... | collective-permute-start | bytes 4325384 | tf_op jit(solution)/shard_map/ppermute | solution.py:119
  705.5 21.3 %all-to-all-start.2 = ((f32[8,8,176]{2,1,0:T(8,128)}), f32[8,8,176]{2,1,0:T(8,128)S(1)}, u32[]{:S(2)}, u32[]{:S(2)}) async-start(f32[8,8,176]{2,1,0:T(8,128)} %gather_fusion.19), calls=%async_computation.2 | async-start | bytes 131072 | tf_op jit(solution)/shard_map/all_to_all | solution.py:123
  710.1 108.2 %collective-permute-start.18 = (bf16[8,176,512]{2,1,0:T(8,128)(2,1)}, bf16[8,176,512]{2,1,0:T(8,128)(2,1)}, u32[]{:S(2)}, u32[]{:S(2)}) collective-permute-start(bf16[8,176,512]{2,1,0:T(8,128)(2,1)} %get-tuple-element.67), channel_id=1, source_target_pairs={{0,33},{1,32},{32,65},{33,64},{64,97},{65,96},{96,1},{97,0},{2,35}... | collective-permute-start | bytes 4325384 | tf_op jit(solution)/shard_map/ppermute | solution.py:119
  714.4 106.6 %collective-permute-start.19 = (bf16[8,176,512]{2,1,0:T(8,128)(2,1)}, bf16[8,176,512]{2,1,0:T(8,128)(2,1)}, u32[]{:S(2)}, u32[]{:S(2)}) collective-permute-start(bf16[8,176,512]{2,1,0:T(8,128)(2,1)} %get-tuple-element.66), channel_id=1, source_target_pairs={{0,64},{1,65},{32,96},{33,97},{64,0},{65,1},{96,32},{97,33},{2,66}... | collective-permute-start | bytes 4325384 | tf_op jit(solution)/shard_map/ppermute | solution.py:119
  716.8 106.7 %collective-permute-start.20 = (bf16[8,176,512]{2,1,0:T(8,128)(2,1)}, bf16[8,176,512]{2,1,0:T(8,128)(2,1)S(1)}, u32[]{:S(2)}, u32[]{:S(2)}) collective-permute-start(bf16[8,176,512]{2,1,0:T(8,128)(2,1)} %get-tuple-element.65), channel_id=1, source_target_pairs={{0,65},{1,64},{32,97},{33,96},{64,1},{65,0},{96,33},{97,32},{2,67}... | collective-permute-start | bytes 4325384 | tf_op jit(solution)/shard_map/ppermute | solution.py:119
  778.2 46.5 %collective-permute-start.21 = (bf16[8,176,512]{2,1,0:T(8,128)(2,1)}, bf16[8,176,512]{2,1,0:T(8,128)(2,1)S(1)}, u32[]{:S(2)}, u32[]{:S(2)}) collective-permute-start(bf16[8,176,512]{2,1,0:T(8,128)(2,1)} %get-tuple-element.70), channel_id=1, source_target_pairs={{0,96},{1,97},{32,0},{33,1},{64,32},{65,33},{96,64},{97,65},{2,98}... | collective-permute-start | bytes 4325384 | tf_op jit(solution)/shard_map/ppermute | solution.py:119
  780.8 61.6 %collective-permute-start.22 = (bf16[8,176,512]{2,1,0:T(8,128)(2,1)S(1)}, bf16[8,176,512]{2,1,0:T(8,128)(2,1)S(1)}, u32[]{:S(2)}, u32[]{:S(2)}) collective-permute-start(bf16[8,176,512]{2,1,0:T(8,128)(2,1)S(1)} %copy-done.12), channel_id=1, source_target_pairs={{0,97},{1,96},{32,1},{33,0},{64,33},{65,32},{96,65},{97,64},{2,99}... | collective-permute-start | bytes 4325384 | tf_op jit(solution)/shard_map/ppermute | solution.py:119
  927.9 20.0 %all-to-all-start.3 = ((f32[4,3,8,8,352]{4,3,2,1,0:T(8,128)}), f32[4,3,8,8,352]{4,3,2,1,0:T(8,128)S(1)}, u32[]{:S(2)}, u32[]{:S(2)}) async-start(f32[4,3,8,8,352]{4,3,2,1,0:T(8,128)} %copy.268), calls=%async_computation.6 | async-start | bytes 2359296 | tf_op jit(solution)/shard_map/all_to_all | solution.py:151
  (29 other events, 371.9 us)
Sparse Core Ops, SparseCore 0:
  11.3 84.5 all-gather.5
  184.0 75.8 all-gather.3
  426.7 145.3 all-reduce.5
  575.3 79.6 reduce-scatter.7
  658.3 81.1 reduce-scatter.3
  742.8 80.7 reduce-scatter.5
